TPU v7x, 32 devices: a whole 2x2x4 slice. The times are simulated.
32 devices in a mesh: obs: 4 (over z), face: 8 (over y, x, core).
Axes of the slice: x: 2, y: 2, z: 4, core: 2. Of those that a mesh axis runs over, the one named last changes fastest.
Arguments:
- density: float32 [34, 8192], P(None, ('obs', 'face')), may hold values from 0.6 to 1.4
- velocity: float32 [3, 34, 8192], P(None, None, ('obs', 'face')), may hold values from -6 to 6
- pressure: float32 [34, 8192], P(None, ('obs', 'face')), may hold values from -6 to 6
- normal: float32 [3, 8192], P(None, ('obs', 'face')), may hold values from -1 to 1, as said below
- direction: float32 [32, 8, 3], P(('obs', 'face')), may hold values from -1 to 1, as said below
- weights: bfloat16 [32, 8, 768, 256], P(('obs', 'face')), may hold values from -0.21875 to 0.21875
- bin_index: int32 [32, 8], P(('obs', 'face')), may hold values from 0 to 7, as said below
- group_index: int32 [32, 8], P(('obs', 'face')), may hold values from 0 to 3
- item_count: int32 [32], P(('obs', 'face')), may hold values from 4 to 8, as said below
Outputs:
- signal: float32 [256, 1024], P('face', 'obs')
Inputs may be any that keep to these rules, and one draw needn't show every extreme that they name: `bin_index`: no time block is named more than 2 times in one device's list; in every draw some device names a block 2 times among its live entries. `item_count`: some device has all 8 entries live. Each face's normal has unit length. Each entry's direction has unit length.
All inputs are finite; a program needn't handle non-finite values.
Results may differ from a plain program's by a relative error of at most 0.0029.
Values sent between devices are 32-bit elements; how exact they have to be, the bound alone decides.
A program may use at most 64 MiB of HBM per device.

v0:
```python
import jax
import jax.numpy as jnp
from jax import lax
from jax.sharding import PartitionSpec as P

SLOT_CAP = 2


def face_terms(dens, veloc, press, norms):
    normal_speed = veloc[0] * norms[0][None] + veloc[1] * norms[1][None] + veloc[2] * norms[2][None]
    flux = dens * normal_speed
    load_first = press * norms[0][None] + dens * veloc[0] * normal_speed
    load_second = press * norms[1][None] + dens * veloc[1] * normal_speed
    load_third = press * norms[2][None] + dens * veloc[2] * normal_speed
    thick = 0.5 * (flux[2:] - flux[:-2])
    return (thick, load_first, load_second, load_third)


def item_source(thick, load_first, load_second, load_third, heading):
    radial = heading[0] * load_first + heading[1] * load_second + heading[2] * load_third
    rate = 0.5 * (radial[2:] - radial[:-2])
    return jnp.concatenate([thick, rate, radial[1:-1]], axis=1).astype(jnp.bfloat16)


def local(
    density, velocity, pressure, normal, direction, weights, bin_index, group_index, item_count
):
    thick, load_first, load_second, load_third = face_terms(density, velocity, pressure, normal)
    headings = direction[0]
    matrices = weights[0]
    blocks_of = bin_index[0]
    groups_of = group_index[0]
    live_count = item_count[0]
    list_total = matrices.shape[0]
    steps = thick.shape[0]
    width = matrices.shape[2]
    n_face = lax.axis_size("face")
    n_obs = lax.axis_size("obs")

    def item_block(listed):
        heading = lax.dynamic_index_in_dim(headings, listed, 0, False)
        source = item_source(thick, load_first, load_second, load_third, heading)
        matrix = lax.dynamic_index_in_dim(matrices, listed, 0, False)
        return jnp.dot(source, matrix, preferred_element_type=jnp.float32)

    order = jnp.arange(list_total, dtype=jnp.int32)
    is_live = order < live_count
    matches = (
        (blocks_of[:, None] == blocks_of[None, :])
        & (order[:, None] > order[None, :])
        & is_live[None, :]
    )
    slot_index = blocks_of * SLOT_CAP + jnp.sum(matches.astype(jnp.int32), axis=1)

    def add_routed(listed, carried):
        outgoing, labels = carried
        target = slot_index[listed]
        outgoing = lax.dynamic_update_index_in_dim(outgoing, item_block(listed)[None], target, 0)
        labels = labels.at[target].set(groups_of[listed].astype(jnp.float32))
        return (outgoing, labels)

    empty_blocks = jnp.zeros((n_face * SLOT_CAP, steps, width), jnp.float32)
    empty_labels = jnp.zeros((n_face * SLOT_CAP,), jnp.float32)
    outgoing, labels = lax.fori_loop(0, live_count, add_routed, (empty_blocks, empty_labels))
    arrived, arrived_labels = (
        lax.all_to_all(
            outgoing.reshape(n_face, SLOT_CAP, steps, width),
            "face",
            split_axis=0,
            concat_axis=0,
            tiled=True,
        ),
        lax.all_to_all(
            labels.reshape(n_face, SLOT_CAP), "face", split_axis=0, concat_axis=0, tiled=True
        ),
    )
    selector = (
        arrived_labels.reshape(1, -1) == jnp.arange(n_obs, dtype=jnp.float32)[:, None]
    ).astype(jnp.float32)
    grouped = jnp.dot(
        selector,
        arrived.reshape(n_face * SLOT_CAP, steps * width),
        precision=lax.Precision.HIGHEST,
        preferred_element_type=jnp.float32,
    )
    owned = lax.psum_scatter(
        grouped.reshape(n_obs, steps, width), "obs", scatter_dimension=0, tiled=True
    )
    return owned.reshape(steps, width)


def solution(mesh):
    placed = (
        P(None, ("obs", "face")),
        P(None, None, ("obs", "face")),
        P(None, ("obs", "face")),
        P(None, ("obs", "face")),
        P(("obs", "face"), None, None),
        P(("obs", "face"), None, None, None),
        P(("obs", "face"), None),
        P(("obs", "face"), None),
        P(("obs", "face")),
    )
    return jax.shard_map(
        local, mesh=mesh, in_specs=placed, out_specs=P("face", "obs"), check_vma=False
    )
```

profile of v0, /device:TPU:0, one launch (start us, length us, event | category | flops | bytes accessed | tf_op | source)
XLA Modules:
  0.0 129.4 jit_solution(2182875037055612578)
XLA Ops:
  7.3 0.9 fusion.17
  8.2 0.9 fusion.20
  10.4 0.9 convert_reduce_fusion
  12.9 67.5 %while.14 = (s32[]{:T(128)}, f32[16,32,256]{2,1,0:T(8,128)}, f32[16]{0:T(128)S(1)}, s32[]{:T(128)}, bf16[32,256]{1,0:T(8,128)(2,1)S(1)}, /*index=5*/f32[8,3]{0,1...) while((s32[]{:T(128)}, f32[16,32,256]{2,1,0:T(8,128)}, ...), condition=%wide.wide.region_2.3_spmd, body=%wide.wide.region_1.2_spmd.sunk | while | flops 12798477 | bytes 729567 | solution.py:64
  14.2 1.8 %multiply_add_fusion.3 = f32[34,256]{1,0:T(8,128)S(1)} fusion(f32[34,256]{1,0:T(8,128)S(1)} %get-tuple-element.300, f32[34,256]{1,0:T(8,128)S(1)} %get-tuple-element.299, f32[34,256]{1,0:T(8,128)S(1)} %get-tuple-element.298, f32[]{:T(128)} %bitcast.83, f32[]{:T(128)} %bitcast.84, f32[]{:T(128)} %bitcast.85), kind=kLoop, calls=%fused_computation.9.clone.1 | loop fusion | flops 43520 | bytes 139276 | tf_op jit(solution)/shard_map/while/body/add | solution.py:20
  18.6 1.8 %fusion.41 = f32[16,32,256]{2,1,0:T(8,128)} fusion(f32[16,32,256]{2,1,0:T(8,128)} %get-tuple-element.275, s32[]{:T(128)S(6)} %select_n.18, bf16[8,768,256]{2,1,0:T(8,128)(2,1)} %get-tuple-element.301, s32[]{:T(128)S(6)} %select_n.17, bf16[32,256]{1,0:T(8,128)(2,1)S(1)} %slice.118, bf16[32,256]{1,0:T(8,128)(2,1)S(1)} %fusion.40, ...), kind=kOutput, calls=%fused_computation.1.clone.1 | convolution fusion | flops 12730368 | bytes 475144 | tf_op jit(solution)/shard_map/while/body/dot_general | solution.py:44
  22.5 1.8 %multiply_add_fusion.3 = f32[34,256]{1,0:T(8,128)S(1)} fusion(f32[34,256]{1,0:T(8,128)S(1)} %get-tuple-element.300, f32[34,256]{1,0:T(8,128)S(1)} %get-tuple-element.299, f32[34,256]{1,0:T(8,128)S(1)} %get-tuple-element.298, f32[]{:T(128)} %bitcast.83, f32[]{:T(128)} %bitcast.84, f32[]{:T(128)} %bitcast.85), kind=kLoop, calls=%fused_computation.9.clone.1 | loop fusion | flops 43520 | bytes 139276 | tf_op jit(solution)/shard_map/while/body/add | solution.py:20
  27.0 1.8 %fusion.41 = f32[16,32,256]{2,1,0:T(8,128)} fusion(f32[16,32,256]{2,1,0:T(8,128)} %get-tuple-element.275, s32[]{:T(128)S(6)} %select_n.18, bf16[8,768,256]{2,1,0:T(8,128)(2,1)} %get-tuple-element.301, s32[]{:T(128)S(6)} %select_n.17, bf16[32,256]{1,0:T(8,128)(2,1)S(1)} %slice.118, bf16[32,256]{1,0:T(8,128)(2,1)S(1)} %fusion.40, ...), kind=kOutput, calls=%fused_computation.1.clone.1 | convolution fusion | flops 12730368 | bytes 475144 | tf_op jit(solution)/shard_map/while/body/dot_general | solution.py:44
  30.9 1.8 %multiply_add_fusion.3 = f32[34,256]{1,0:T(8,128)S(1)} fusion(f32[34,256]{1,0:T(8,128)S(1)} %get-tuple-element.300, f32[34,256]{1,0:T(8,128)S(1)} %get-tuple-element.299, f32[34,256]{1,0:T(8,128)S(1)} %get-tuple-element.298, f32[]{:T(128)} %bitcast.83, f32[]{:T(128)} %bitcast.84, f32[]{:T(128)} %bitcast.85), kind=kLoop, calls=%fused_computation.9.clone.1 | loop fusion | flops 43520 | bytes 139276 | tf_op jit(solution)/shard_map/while/body/add | solution.py:20
  35.3 1.8 %fusion.41 = f32[16,32,256]{2,1,0:T(8,128)} fusion(f32[16,32,256]{2,1,0:T(8,128)} %get-tuple-element.275, s32[]{:T(128)S(6)} %select_n.18, bf16[8,768,256]{2,1,0:T(8,128)(2,1)} %get-tuple-element.301, s32[]{:T(128)S(6)} %select_n.17, bf16[32,256]{1,0:T(8,128)(2,1)S(1)} %slice.118, bf16[32,256]{1,0:T(8,128)(2,1)S(1)} %fusion.40, ...), kind=kOutput, calls=%fused_computation.1.clone.1 | convolution fusion | flops 12730368 | bytes 475144 | tf_op jit(solution)/shard_map/while/body/dot_general | solution.py:44
  39.3 1.8 %multiply_add_fusion.3 = f32[34,256]{1,0:T(8,128)S(1)} fusion(f32[34,256]{1,0:T(8,128)S(1)} %get-tuple-element.300, f32[34,256]{1,0:T(8,128)S(1)} %get-tuple-element.299, f32[34,256]{1,0:T(8,128)S(1)} %get-tuple-element.298, f32[]{:T(128)} %bitcast.83, f32[]{:T(128)} %bitcast.84, f32[]{:T(128)} %bitcast.85), kind=kLoop, calls=%fused_computation.9.clone.1 | loop fusion | flops 43520 | bytes 139276 | tf_op jit(solution)/shard_map/while/body/add | solution.py:20
  43.7 1.8 %fusion.41 = f32[16,32,256]{2,1,0:T(8,128)} fusion(f32[16,32,256]{2,1,0:T(8,128)} %get-tuple-element.275, s32[]{:T(128)S(6)} %select_n.18, bf16[8,768,256]{2,1,0:T(8,128)(2,1)} %get-tuple-element.301, s32[]{:T(128)S(6)} %select_n.17, bf16[32,256]{1,0:T(8,128)(2,1)S(1)} %slice.118, bf16[32,256]{1,0:T(8,128)(2,1)S(1)} %fusion.40, ...), kind=kOutput, calls=%fused_computation.1.clone.1 | convolution fusion | flops 12730368 | bytes 475144 | tf_op jit(solution)/shard_map/while/body/dot_general | solution.py:44
  47.6 1.8 %multiply_add_fusion.3 = f32[34,256]{1,0:T(8,128)S(1)} fusion(f32[34,256]{1,0:T(8,128)S(1)} %get-tuple-element.300, f32[34,256]{1,0:T(8,128)S(1)} %get-tuple-element.299, f32[34,256]{1,0:T(8,128)S(1)} %get-tuple-element.298, f32[]{:T(128)} %bitcast.83, f32[]{:T(128)} %bitcast.84, f32[]{:T(128)} %bitcast.85), kind=kLoop, calls=%fused_computation.9.clone.1 | loop fusion | flops 43520 | bytes 139276 | tf_op jit(solution)/shard_map/while/body/add | solution.py:20
  52.0 1.8 %fusion.41 = f32[16,32,256]{2,1,0:T(8,128)} fusion(f32[16,32,256]{2,1,0:T(8,128)} %get-tuple-element.275, s32[]{:T(128)S(6)} %select_n.18, bf16[8,768,256]{2,1,0:T(8,128)(2,1)} %get-tuple-element.301, s32[]{:T(128)S(6)} %select_n.17, bf16[32,256]{1,0:T(8,128)(2,1)S(1)} %slice.118, bf16[32,256]{1,0:T(8,128)(2,1)S(1)} %fusion.40, ...), kind=kOutput, calls=%fused_computation.1.clone.1 | convolution fusion | flops 12730368 | bytes 475144 | tf_op jit(solution)/shard_map/while/body/dot_general | solution.py:44
  56.0 1.8 %multiply_add_fusion.3 = f32[34,256]{1,0:T(8,128)S(1)} fusion(f32[34,256]{1,0:T(8,128)S(1)} %get-tuple-element.300, f32[34,256]{1,0:T(8,128)S(1)} %get-tuple-element.299, f32[34,256]{1,0:T(8,128)S(1)} %get-tuple-element.298, f32[]{:T(128)} %bitcast.83, f32[]{:T(128)} %bitcast.84, f32[]{:T(128)} %bitcast.85), kind=kLoop, calls=%fused_computation.9.clone.1 | loop fusion | flops 43520 | bytes 139276 | tf_op jit(solution)/shard_map/while/body/add | solution.py:20
  60.4 1.8 %fusion.41 = f32[16,32,256]{2,1,0:T(8,128)} fusion(f32[16,32,256]{2,1,0:T(8,128)} %get-tuple-element.275, s32[]{:T(128)S(6)} %select_n.18, bf16[8,768,256]{2,1,0:T(8,128)(2,1)} %get-tuple-element.301, s32[]{:T(128)S(6)} %select_n.17, bf16[32,256]{1,0:T(8,128)(2,1)S(1)} %slice.118, bf16[32,256]{1,0:T(8,128)(2,1)S(1)} %fusion.40, ...), kind=kOutput, calls=%fused_computation.1.clone.1 | convolution fusion | flops 12730368 | bytes 475144 | tf_op jit(solution)/shard_map/while/body/dot_general | solution.py:44
  64.3 1.8 %multiply_add_fusion.3 = f32[34,256]{1,0:T(8,128)S(1)} fusion(f32[34,256]{1,0:T(8,128)S(1)} %get-tuple-element.300, f32[34,256]{1,0:T(8,128)S(1)} %get-tuple-element.299, f32[34,256]{1,0:T(8,128)S(1)} %get-tuple-element.298, f32[]{:T(128)} %bitcast.83, f32[]{:T(128)} %bitcast.84, f32[]{:T(128)} %bitcast.85), kind=kLoop, calls=%fused_computation.9.clone.1 | loop fusion | flops 43520 | bytes 139276 | tf_op jit(solution)/shard_map/while/body/add | solution.py:20
  68.8 1.8 %fusion.41 = f32[16,32,256]{2,1,0:T(8,128)} fusion(f32[16,32,256]{2,1,0:T(8,128)} %get-tuple-element.275, s32[]{:T(128)S(6)} %select_n.18, bf16[8,768,256]{2,1,0:T(8,128)(2,1)} %get-tuple-element.301, s32[]{:T(128)S(6)} %select_n.17, bf16[32,256]{1,0:T(8,128)(2,1)S(1)} %slice.118, bf16[32,256]{1,0:T(8,128)(2,1)S(1)} %fusion.40, ...), kind=kOutput, calls=%fused_computation.1.clone.1 | convolution fusion | flops 12730368 | bytes 475144 | tf_op jit(solution)/shard_map/while/body/dot_general | solution.py:44
  72.7 1.8 %multiply_add_fusion.3 = f32[34,256]{1,0:T(8,128)S(1)} fusion(f32[34,256]{1,0:T(8,128)S(1)} %get-tuple-element.300, f32[34,256]{1,0:T(8,128)S(1)} %get-tuple-element.299, f32[34,256]{1,0:T(8,128)S(1)} %get-tuple-element.298, f32[]{:T(128)} %bitcast.83, f32[]{:T(128)} %bitcast.84, f32[]{:T(128)} %bitcast.85), kind=kLoop, calls=%fused_computation.9.clone.1 | loop fusion | flops 43520 | bytes 139276 | tf_op jit(solution)/shard_map/while/body/add | solution.py:20
  77.1 1.8 %fusion.41 = f32[16,32,256]{2,1,0:T(8,128)} fusion(f32[16,32,256]{2,1,0:T(8,128)} %get-tuple-element.275, s32[]{:T(128)S(6)} %select_n.18, bf16[8,768,256]{2,1,0:T(8,128)(2,1)} %get-tuple-element.301, s32[]{:T(128)S(6)} %select_n.17, bf16[32,256]{1,0:T(8,128)(2,1)S(1)} %slice.118, bf16[32,256]{1,0:T(8,128)(2,1)S(1)} %fusion.40, ...), kind=kOutput, calls=%fused_computation.1.clone.1 | convolution fusion | flops 12730368 | bytes 475144 | tf_op jit(solution)/shard_map/while/body/dot_general | solution.py:44
  80.5 8.7 %all_to_all.14 = f32[8,1,2]{2,1,0:T(1,128)S(1)} all-to-all(f32[8,1,2]{2,1,0:T(1,128)S(1)} %bitcast.91), channel_id=1, replica_groups=mesh['obs'=4,'face'=8] {'face'}, dimensions={0} | all-to-all | bytes 128 | tf_op jit(solution)/shard_map/all_to_all | solution.py:73
  89.2 3.5 %all-to-all-start.1 = ((f32[8,2,32,256]{3,2,1,0:T(8,128)}), f32[8,2,32,256]{3,2,1,0:T(8,128)S(1)}, u32[]{:S(2)}, u32[]{:S(2)}) async-start(f32[8,2,32,256]{3,2,1,0:T(8,128)} %bitcast.12), calls=%async_computation.1 | async-start | bytes 1048576 | tf_op jit(solution)/shard_map/all_to_all | solution.py:66
  94.0 8.3 %all-to-all-done.1 = f32[8,2,32,256]{3,2,1,0:T(8,128)S(1)} async-done(((f32[8,2,32,256]{3,2,1,0:T(8,128)}), f32[8,2,32,256]{3,2,1,0:T(8,128)S(1)}, u32[]{:S(2)}, u32[]{:S(2)}) %all-to-all-start.1) | async-done | bytes 524320 | tf_op jit(solution)/shard_map/all_to_all | solution.py:66
  103.7 18.9 %reduce-scatter.2.cloned.1.call-done = f32[1,32,256]{2,1,0:T(8,128)} async-done(((f32[4,32,256]{2,1,0:T(8,128)}), f32[1,32,256]{2,1,0:T(8,128)}) %reduce-scatter.2.cloned.1.call-update) | async-done | bytes 32784 | tf_op jit(solution)/shard_map/reduce_scatter | solution.py:86
  (63 shorter events, 22.8 us)
Async XLA Ops:
  89.2 13.1 %all-to-all-start.1 = ((f32[8,2,32,256]{3,2,1,0:T(8,128)}), f32[8,2,32,256]{3,2,1,0:T(8,128)S(1)}, u32[]{:S(2)}, u32[]{:S(2)}) async-start(f32[8,2,32,256]{3,2,1,0:T(8,128)} %bitcast.12), calls=%async_computation.1 | async-start | bytes 1048576 | tf_op jit(solution)/shard_map/all_to_all | solution.py:66
  92.7 29.9 %reduce-scatter.2.cloned.1.call-start = ((), (), s32[]{:S(2)}) async-start(), calls=%async_computation.3 | async-start | bytes 163840 | tf_op jit(solution)/shard_map/reduce_scatter | solution.py:86
Sparse Core Ops, SparseCore 0:
  103.8 18.7 reduce-scatter.1
where the time goes:
time: 131 us; the launch traced here: 129 us
  waiting for transfers between devices  27.3 us (21%)
  other arithmetic  25 us (19%)
  loops' own time  21.5 us (16%)
  matrix products  15 us (11%)
  local copies, waits for them, and re-layouts  14.2 us (11%)
  between operations  14.1 us (11%)
  blocking collectives  8.75 us (7%)
  starting transfers between devices  3.53 us (3%)
    another operation x1, loops' own time, local(): lax.fori_loop(0, live_count, add_routed, (empty_blocks, empty_labels))  21.5 us
    reduce_scatter x1, waiting for transfers between devices, local(): lax.psum_scatter(grouped.reshape(n_obs, steps, width), 'obs', scatter_dim...  18.9 us
    add x8, other arithmetic, item_source(): heading[0] * load_first + heading[1] * load_second + heading[2] * load_third  14.5 us
    dot_general x8, matrix products, item_block(): return jnp.dot(source, matrix, preferred_element_type=jnp.float32)  14.4 us
    all_to_all x1, blocking collectives, local(): lax.all_to_all(labels.reshape(n_face, SLOT_CAP), 'face', split_axis=0, co...  8.75 us
    all_to_all x1, waiting for transfers between devices, local(): lax.all_to_all(outgoing.reshape(n_face, SLOT_CAP, steps, width), 'face',...  8.34 us
    scatter x8, other arithmetic, add_routed(): labels = labels.at[target].set(groups_of[listed].astype(jnp.float32))  6.47 us
    dynamic_slice x8, local copies, waits for them, and re-layouts, add_routed(): target = slot_index[listed]  5.26 us
  transfers between devices with their start and end apart: 2, of which 2 were waited for; matrix products, arithmetic and copies ran while one was open for 1% of the time, Pallas kernels for 0%

commit v1 on v0

v1 whole, which is shorter than its diff:
```python
import functools

import jax
import jax.numpy as jnp
from jax import lax
from jax.experimental import pallas as pl
from jax.experimental.pallas import tpu as pltpu
from jax.sharding import PartitionSpec as P

SLOT_CAP = 2
MESH = pl.DeviceIdType.MESH


def loop(first, last, body):
    if last - first <= 8:
        for at in range(first, last):
            body(at)
    else:
        lax.fori_loop(first, last, lambda at, _: (body(at), _)[1], 0)


def kernel(
    n_obs, n_face, chunks,
    direction, bin_index, group_index, item_count,
    density, velocity, pressure, normal, weights,
    out,
    dens, veloc, press, norms, matrices, thick, rate_of, load_of, blocks,
    outgoing, arrived, labels_out, labels_in, grouped, owned,
    in_sem, weight_sem, label_send, label_recv, send_sem, recv_sem, send_two, recv_two,
):
    my_obs, my_face = lax.axis_index("obs"), lax.axis_index("face")
    list_total = matrices.shape[0]
    steps, width = thick.shape
    part = width // chunks

    loads = [
        pltpu.make_async_copy(density, dens, in_sem.at[0]),
        pltpu.make_async_copy(velocity, veloc, in_sem.at[1]),
        pltpu.make_async_copy(pressure, press, in_sem.at[2]),
        pltpu.make_async_copy(normal, norms, in_sem.at[3]),
    ]
    for copy in loads:
        copy.start()

    def weight_copy(listed):
        return pltpu.make_async_copy(
            weights.at[0, listed], matrices.at[listed], weight_sem.at[listed]
        )

    loop(0, list_total, lambda listed: weight_copy(listed).start())

    barrier = pltpu.get_barrier_semaphore()

    def greet_face(shift):
        peer = lax.rem(my_face + shift, n_face)
        pl.semaphore_signal(barrier, inc=1, device_id=(my_obs, peer), device_id_type=MESH)

    def greet_obs(shift):
        peer = lax.rem(my_obs + shift, n_obs)
        pl.semaphore_signal(barrier, inc=1, device_id=(peer, my_face), device_id_type=MESH)

    loop(1, n_face, greet_face)
    loop(1, n_obs, greet_obs)

    live_count = item_count[0]

    def slots_of(block):
        last = jnp.int32(-1)
        first = jnp.int32(-1)
        for listed in range(list_total):
            match = (bin_index[0, listed] == block) & (listed < live_count)
            last = jnp.where(match, listed, last)
        for listed in reversed(range(list_total)):
            match = (bin_index[0, listed] == block) & (listed < live_count)
            first = jnp.where(match, listed, first)
        return first, last

    upper = lax.broadcasted_iota(jnp.int32, labels_out.shape[1:], 0) < 4

    def fill_labels(block):
        first, last = slots_of(block)
        label_first = group_index[0, jnp.maximum(first, 0)]
        label_last = group_index[0, jnp.maximum(last, 0)]
        return jnp.where(upper, label_first, label_last)

    def label_copy(shift):
        peer = lax.rem(my_face + shift, n_face)
        return pltpu.make_async_remote_copy(
            src_ref=labels_out.at[peer],
            dst_ref=labels_in.at[my_face],
            send_sem=label_send.at[shift - 1],
            recv_sem=label_recv.at[shift - 1],
            device_id=(my_obs, peer),
            device_id_type=MESH,
        )

    def set_label(shift):
        peer = lax.rem(my_face + shift, n_face)
        labels_out[peer] = fill_labels(peer)

    loop(1, n_face, set_label)
    pl.semaphore_wait(barrier, n_face + n_obs - 2)
    loop(1, n_face, lambda shift: label_copy(shift).start())

    for copy in loads:
        copy.wait()
    n0, n1, n2 = norms[0:1], norms[1:2], norms[2:3]
    v0, v1, v2 = veloc[0], veloc[1], veloc[2]
    density_now, pressure_now = dens[...], press[...]
    normal_speed = v0 * n0 + v1 * n1 + v2 * n2
    flux = density_now * normal_speed
    thick[...] = (0.5 * (flux[2:] - flux[:-2])).astype(jnp.bfloat16)
    for c, (n, v) in enumerate(((n0, v0), (n1, v1), (n2, v2))):
        load = pressure_now * n + density_now * v * normal_speed
        rate_of[c] = 0.5 * (load[2:] - load[:-2])
        load_of[c] = load[1:-1]

    def compute(listed):
        h0, h1, h2 = (direction[0, listed, c] for c in range(3))
        rate = h0 * rate_of[0] + h1 * rate_of[1] + h2 * rate_of[2]
        radial = h0 * load_of[0] + h1 * load_of[1] + h2 * load_of[2]
        source = jnp.concatenate(
            [thick[...], rate.astype(jnp.bfloat16), radial.astype(jnp.bfloat16)], axis=1
        )
        weight_copy(listed).wait()
        blocks[listed] = jnp.dot(source, matrices[listed], preferred_element_type=jnp.float32)

    loop(0, list_total, compute)

    def data_copy(chunk, shift):
        peer = lax.rem(my_face + shift, n_face)
        return pltpu.make_async_remote_copy(
            src_ref=outgoing.at[chunk, peer],
            dst_ref=arrived.at[chunk, my_face],
            send_sem=send_sem.at[chunk, shift - 1],
            recv_sem=recv_sem.at[chunk, shift - 1],
            device_id=(my_obs, peer),
            device_id_type=MESH,
        )

    def route(chunk, block):
        first, last = slots_of(block)
        columns = pl.ds(chunk * part, part)
        early = blocks[jnp.maximum(first, 0), :, columns]
        late = blocks[jnp.maximum(last, 0), :, columns]
        return jnp.where(last >= 0, early, 0.0), jnp.where(last > first, late, 0.0)

    for chunk in range(chunks):
        def send(shift):
            peer = lax.rem(my_face + shift, n_face)
            early, late = route(chunk, peer)
            outgoing[chunk, peer, :steps] = early
            outgoing[chunk, peer, steps:] = late
            data_copy(chunk, shift).start()

        loop(1, n_face, send)

    def selected(early, late, label_first, label_last):
        return [
            jnp.where(label_first == group, early, 0.0) + jnp.where(label_last == group, late, 0.0)
            for group in range(n_obs)
        ]

    def obs_copy(chunk, shift):
        peer = lax.rem(my_obs + shift, n_obs)
        return pltpu.make_async_remote_copy(
            src_ref=grouped.at[chunk, peer],
            dst_ref=owned.at[chunk, my_obs],
            send_sem=send_two.at[chunk, shift - 1],
            recv_sem=recv_two.at[chunk, shift - 1],
            device_id=(peer, my_face),
            device_id_type=MESH,
        )

    own_labels = fill_labels(my_face)
    for chunk in range(chunks):
        early, late = route(chunk, my_face)
        sums = tuple(selected(early, late, own_labels[0:1], own_labels[4:5]))

        def collect(shift, sums, chunk=chunk):
            source = lax.rem(my_face + n_face - shift, n_face)
            if chunk == 0:
                label_copy(shift).wait_recv()
            data_copy(chunk, shift).wait_recv()
            labels = labels_in[source]
            both = arrived[chunk, source]
            terms = selected(both[:steps], both[steps:], labels[0:1], labels[4:5])
            return tuple(a + b for a, b in zip(sums, terms))

        if n_face <= 8:
            for shift in range(1, n_face):
                sums = collect(shift, sums)
        else:
            sums = lax.fori_loop(1, n_face, collect, sums)
        for group in range(n_obs):
            grouped[chunk, group] = sums[group]
        loop(1, n_obs, lambda shift: obs_copy(chunk, shift).start())

    for chunk in range(chunks):
        total = grouped[chunk, my_obs]
        for shift in range(1, n_obs):
            source = lax.rem(my_obs + n_obs - shift, n_obs)
            obs_copy(chunk, shift).wait_recv()
            total = total + owned[chunk, source]
        out[:, chunk * part:(chunk + 1) * part] = total

    for chunk in range(chunks):
        loop(1, n_face, lambda shift: data_copy(chunk, shift).wait_send())
        loop(1, n_obs, lambda shift: obs_copy(chunk, shift).wait_send())
    loop(1, n_face, lambda shift: label_copy(shift).wait_send())


def local(
    density, velocity, pressure, normal, direction, weights, bin_index, group_index, item_count
):
    n_face, n_obs = lax.axis_size("face"), lax.axis_size("obs")
    list_total, depth, width = weights.shape[1:]
    rows, faces = density.shape
    steps = rows - 2
    chunks = max(1, width // 128)
    part = width // chunks
    smem = pl.BlockSpec(memory_space=pltpu.SMEM)
    anywhere = pl.BlockSpec(memory_space=pl.ANY)
    f32 = jnp.float32
    return pl.pallas_call(
        functools.partial(kernel, n_obs, n_face, chunks),
        out_shape=jax.ShapeDtypeStruct((steps, width), f32),
        in_specs=[smem] * 4 + [anywhere] * 5,
        out_specs=pl.BlockSpec(memory_space=pltpu.VMEM),
        scratch_shapes=[
            pltpu.VMEM((rows, faces), f32),
            pltpu.VMEM((3, rows, faces), f32),
            pltpu.VMEM((rows, faces), f32),
            pltpu.VMEM((3, faces), f32),
            pltpu.VMEM((list_total, depth, width), jnp.bfloat16),
            pltpu.VMEM((steps, faces), jnp.bfloat16),
            pltpu.VMEM((3, steps, faces), f32),
            pltpu.VMEM((3, steps, faces), f32),
            pltpu.VMEM((list_total, steps, width), f32),
            pltpu.VMEM((chunks, n_face, SLOT_CAP * steps, part), f32),
            pltpu.VMEM((chunks, n_face, SLOT_CAP * steps, part), f32),
            pltpu.VMEM((n_face, 8, 128), jnp.int32),
            pltpu.VMEM((n_face, 8, 128), jnp.int32),
            pltpu.VMEM((chunks, n_obs, steps, part), f32),
            pltpu.VMEM((chunks, n_obs, steps, part), f32),
            pltpu.SemaphoreType.DMA((4,)),
            pltpu.SemaphoreType.DMA((list_total,)),
            pltpu.SemaphoreType.DMA((n_face - 1,)),
            pltpu.SemaphoreType.DMA((n_face - 1,)),
            pltpu.SemaphoreType.DMA((chunks, n_face - 1)),
            pltpu.SemaphoreType.DMA((chunks, n_face - 1)),
            pltpu.SemaphoreType.DMA((chunks, n_obs - 1)),
            pltpu.SemaphoreType.DMA((chunks, n_obs - 1)),
        ],
        compiler_params=pltpu.CompilerParams(
            collective_id=0, has_side_effects=True
        ),
    )(
        direction, bin_index, group_index, item_count,
        density, velocity, pressure, normal, weights,
    )


def solution(mesh):
    placed = (
        P(None, ("obs", "face")),
        P(None, None, ("obs", "face")),
        P(None, ("obs", "face")),
        P(None, ("obs", "face")),
        P(("obs", "face"), None, None),
        P(("obs", "face"), None, None, None),
        P(("obs", "face"), None),
        P(("obs", "face"), None),
        P(("obs", "face")),
    )
    return jax.shard_map(
        local, mesh=mesh, in_specs=placed, out_specs=P("face", "obs"), check_vma=False
    )
```

time: 131 us -> 23.7 us (0.18); the launches traced: 129 us -> 23.5 us
  waiting for transfers between devices: 27.3 us -> 0 us
  other arithmetic: 25 us -> 0 us
  loops' own time: 21.5 us -> 0 us
  Pallas kernels: 0 us -> 20.1 us
  matrix products: 15 us -> 0 us
  between operations: 14.1 us -> 0.66 us
  local copies, waits for them, and re-layouts: 14.2 us -> 2.72 us
  blocking collectives: 8.75 us -> 0 us
  starting transfers between devices: 3.53 us -> 0 us
    another operation x1 -> x0, loops' own time: 21.5 us -> none  [local(): lax.fori_loop(0, live_count, add_routed, (empty_blocks, empty_labels))]
    pallas_call x0 -> x1, Pallas kernels: none -> 20.1 us  [local(): pl.pallas_call(functools.partial(kernel, n_obs, n_face, chunks), out_shap...]
    reduce_scatter x1 -> x0, waiting for transfers between devices: 18.9 us -> none  [local(): lax.psum_scatter(grouped.reshape(n_obs, steps, width), 'obs', scatter_dim...]
    add x11 -> x0, other arithmetic: 16.9 us -> none  [the longest x8 14.5 us: item_source(): heading[0] * load_first + heading[1] * load_second + heading[2] * load_third]
    dot_general x9 -> x0, matrix products: 15 us -> none  [the longest x8 14.4 us: item_block(): return jnp.dot(source, matrix, preferred_element_type=jnp.float32)]
    all_to_all x1 -> x0, blocking collectives: 8.75 us -> none  [local(): lax.all_to_all(labels.reshape(n_face, SLOT_CAP), 'face', split_axis=0, co...]
    all_to_all x1 -> x0, waiting for transfers between devices: 8.34 us -> none  [local(): lax.all_to_all(outgoing.reshape(n_face, SLOT_CAP, steps, width), 'face',...]
    scatter x8 -> x0, other arithmetic: 6.47 us -> none  [add_routed(): labels = labels.at[target].set(groups_of[listed].astype(jnp.float32))]
  transfers between devices with their start and end apart: 2 -> 0, of which waited for: 2 -> 0; matrix products, arithmetic and copies ran while one was open for 1% -> 0% of each run, Pallas kernels for 0% -> 0%
where the time goes in v1:
time: 23.7 us; the launch traced here: 23.5 us
  Pallas kernels  20.1 us (85%)
  local copies, waits for them, and re-layouts  2.72 us (11%)
  between operations  0.66 us (3%)
    pallas_call x1, Pallas kernels, local(): pl.pallas_call(functools.partial(kernel, n_obs, n_face, chunks), out_shap...  20.1 us
    unnamed x2, local copies, waits for them, and re-layouts  2.72 us

profile of v1, /device:TPU:0, one launch (start us, length us, event | category | flops | bytes accessed | tf_op | source)
XLA Modules:
  0.0 23.5 jit_solution(17217866106780048008)
XLA Ops:
  0.7 1.3 %copy.10.direction = f32[1,8,3]{2,1,0:T(8,128)} copy(f32[1,8,3]{1,0,2:T(1,128)} %param.13) | data formatting | bytes 192 | tf_op args[4]
  2.0 20.1 %shard_map.91 = f32[32,256]{1,0:T(8,128)} custom-call(f32[1,8,3]{2,1,0:T(8,128)} %copy.10.direction, s32[1,8]{1,0:T(1,128)} %bin_index.1, s32[1,8]{1,0:T(1,128)} %group_index.1, s32[1]{0:T(128)S(6)} %copy.12.item_count, f32[34,256]{1,0:T(8,128)} %density.1, f32[3,34,256]{2,1,0:T(8,128)} %velocity.1, f32[34,256]{1,0:T(8,128)} %pressure.1, f32[3,256]{1,0:T(4,128)} %normal.1, ...), custom_call_target="tpu_custom_call" | custom-call | tf_op jit(solution)/shard_map/pallas_call | solution.py:225
  22.1 1.4 %copy.13 = f32[32,256]{1,0:T(8,128)} copy(f32[32,256]{1,0:T(8,128)} %shard_map.91) | data formatting | bytes 65536

commit v2 on v1

--- a/solution.py
+++ b/solution.py
@@ -24,12 +24,12 @@
     direction, bin_index, group_index, item_count,
     density, velocity, pressure, normal, weights,
     out,
-    dens, veloc, press, norms, matrices, thick, rate_of, load_of, blocks,
+    dens, veloc, press, norms, matrices, thick, rate_of, load_of, sources, blocks,
     outgoing, arrived, labels_out, labels_in, grouped, owned,
     in_sem, weight_sem, label_send, label_recv, send_sem, recv_sem, send_two, recv_two,
 ):
     my_obs, my_face = lax.axis_index("obs"), lax.axis_index("face")
-    list_total = matrices.shape[0]
+    list_total = matrices.shape[1]
     steps, width = thick.shape
     part = width // chunks
 
@@ -42,12 +42,15 @@
     for copy in loads:
         copy.start()
 
-    def weight_copy(listed):
+    def weight_copy(chunk, listed):
         return pltpu.make_async_copy(
-            weights.at[0, listed], matrices.at[listed], weight_sem.at[listed]
-        )
-
-    loop(0, list_total, lambda listed: weight_copy(listed).start())
+            weights.at[0, listed, :, pl.ds(chunk * part, part)],
+            matrices.at[chunk, listed],
+            weight_sem.at[chunk, listed],
+        )
+
+    for chunk in range(chunks):
+        loop(0, list_total, lambda listed: weight_copy(chunk, listed).start())
 
     barrier = pltpu.get_barrier_semaphore()
 
@@ -99,8 +102,6 @@
         labels_out[peer] = fill_labels(peer)
 
     loop(1, n_face, set_label)
-    pl.semaphore_wait(barrier, n_face + n_obs - 2)
-    loop(1, n_face, lambda shift: label_copy(shift).start())
 
     for copy in loads:
         copy.wait()
@@ -115,17 +116,23 @@
         rate_of[c] = 0.5 * (load[2:] - load[:-2])
         load_of[c] = load[1:-1]
 
-    def compute(listed):
-        h0, h1, h2 = (direction[0, listed, c] for c in range(3))
+    def prepare(listed):
+        h0, h1, h2 = (direction[c, 0, listed] for c in range(3))
         rate = h0 * rate_of[0] + h1 * rate_of[1] + h2 * rate_of[2]
         radial = h0 * load_of[0] + h1 * load_of[1] + h2 * load_of[2]
-        source = jnp.concatenate(
+        sources[listed] = jnp.concatenate(
             [thick[...], rate.astype(jnp.bfloat16), radial.astype(jnp.bfloat16)], axis=1
         )
-        weight_copy(listed).wait()
-        blocks[listed] = jnp.dot(source, matrices[listed], preferred_element_type=jnp.float32)
-
-    loop(0, list_total, compute)
+
+    loop(0, list_total, prepare)
+    pl.semaphore_wait(barrier, n_face + n_obs - 2)
+    loop(1, n_face, lambda shift: label_copy(shift).start())
+
+    def compute(chunk, listed):
+        weight_copy(chunk, listed).wait()
+        blocks[chunk, listed] = jnp.dot(
+            sources[listed], matrices[chunk, listed], preferred_element_type=jnp.float32
+        )
 
     def data_copy(chunk, shift):
         peer = lax.rem(my_face + shift, n_face)
@@ -140,12 +147,13 @@
 
     def route(chunk, block):
         first, last = slots_of(block)
-        columns = pl.ds(chunk * part, part)
-        early = blocks[jnp.maximum(first, 0), :, columns]
-        late = blocks[jnp.maximum(last, 0), :, columns]
+        early = blocks[chunk, jnp.maximum(first, 0)]
+        late = blocks[chunk, jnp.maximum(last, 0)]
         return jnp.where(last >= 0, early, 0.0), jnp.where(last > first, late, 0.0)
 
     for chunk in range(chunks):
+        loop(0, list_total, functools.partial(compute, chunk))
+
         def send(shift):
             peer = lax.rem(my_face + shift, n_face)
             early, late = route(chunk, peer)
@@ -224,7 +232,7 @@
     f32 = jnp.float32
     return pl.pallas_call(
         functools.partial(kernel, n_obs, n_face, chunks),
-        out_shape=jax.ShapeDtypeStruct((steps, width), f32),
+        out_shape=pltpu.VMEM((steps, width), f32),
         in_specs=[smem] * 4 + [anywhere] * 5,
         out_specs=pl.BlockSpec(memory_space=pltpu.VMEM),
         scratch_shapes=[
@@ -232,19 +240,20 @@
             pltpu.VMEM((3, rows, faces), f32),
             pltpu.VMEM((rows, faces), f32),
             pltpu.VMEM((3, faces), f32),
-            pltpu.VMEM((list_total, depth, width), jnp.bfloat16),
+            pltpu.VMEM((chunks, list_total, depth, part), jnp.bfloat16),
             pltpu.VMEM((steps, faces), jnp.bfloat16),
             pltpu.VMEM((3, steps, faces), f32),
             pltpu.VMEM((3, steps, faces), f32),
-            pltpu.VMEM((list_total, steps, width), f32),
+            pltpu.VMEM((list_total, steps, depth), jnp.bfloat16),
+            pltpu.VMEM((chunks, list_total, steps, part), f32),
             pltpu.VMEM((chunks, n_face, SLOT_CAP * steps, part), f32),
             pltpu.VMEM((chunks, n_face, SLOT_CAP * steps, part), f32),
-            pltpu.VMEM((n_face, 8, 128), jnp.int32),
-            pltpu.VMEM((n_face, 8, 128), jnp.int32),
+            pltpu.VMEM((n_face, 8, part), jnp.int32),
+            pltpu.VMEM((n_face, 8, part), jnp.int32),
             pltpu.VMEM((chunks, n_obs, steps, part), f32),
             pltpu.VMEM((chunks, n_obs, steps, part), f32),
             pltpu.SemaphoreType.DMA((4,)),
-            pltpu.SemaphoreType.DMA((list_total,)),
+            pltpu.SemaphoreType.DMA((chunks, list_total)),
             pltpu.SemaphoreType.DMA((n_face - 1,)),
             pltpu.SemaphoreType.DMA((n_face - 1,)),
             pltpu.SemaphoreType.DMA((chunks, n_face - 1)),
@@ -256,7 +265,7 @@
             collective_id=0, has_side_effects=True
         ),
     )(
-        direction, bin_index, group_index, item_count,
+        jnp.transpose(direction, (2, 0, 1)), bin_index, group_index, item_count,
         density, velocity, pressure, normal, weights,
     )
 

time: 23.7 us -> 20.8 us (0.88)
  local copies, waits for them, and re-layouts: 2.72 us -> 0.62 us
  Pallas kernels: 20.1 us -> 19.3 us
    unnamed x2 -> x1, local copies, waits for them, and re-layouts: 2.72 us -> 0.62 us
    pallas_call x1, Pallas kernels: 20.1 us -> 19.3 us  [local(): pl.pallas_call(functools.partial(kernel, n_obs, n_face, chunks), out_shap...]
where the time goes in v2:
time: 20.8 us; the launch traced here: 20.6 us
  Pallas kernels  19.3 us (93%)
  between operations  0.66 us (3%)
  local copies, waits for them, and re-layouts  0.62 us (3%)
    pallas_call x1, Pallas kernels, local(): pl.pallas_call(functools.partial(kernel, n_obs, n_face, chunks), out_shap...  19.3 us
    unnamed x1, local copies, waits for them, and re-layouts  0.62 us

profile of v2, /device:TPU:0, one launch (start us, length us, event | category | flops | bytes accessed | tf_op | source)
XLA Modules:
  0.0 20.6 jit_solution(18147927255091135455)
XLA Ops:
  0.7 19.3 %shard_map.91 = f32[32,256]{1,0:T(8,128)S(1)} custom-call(f32[3,1,8]{2,1,0:T(1,128)} %bitcast.1, s32[1,8]{1,0:T(1,128)} %bin_index.1, s32[1,8]{1,0:T(1,128)} %group_index.1, s32[1]{0:T(128)S(6)} %copy.12.item_count, f32[34,256]{1,0:T(8,128)} %density.1, f32[3,34,256]{2,1,0:T(8,128)} %velocity.1, f32[34,256]{1,0:T(8,128)} %pressure.1, f32[3,256]{1,0:T(4,128)} %normal.1, ...), custom_call_target="tpu_custom_call" | custom-call | tf_op jit(solution)/shard_map/pallas_call | solution.py:233
  20.0 0.6 %copy.11 = f32[32,256]{1,0:T(8,128)} copy(f32[32,256]{1,0:T(8,128)S(1)} %shard_map.91) | data formatting | bytes 65536

commit v3 on v2

--- a/solution.py
+++ b/solution.py
@@ -128,11 +128,18 @@
     pl.semaphore_wait(barrier, n_face + n_obs - 2)
     loop(1, n_face, lambda shift: label_copy(shift).start())
 
-    def compute(chunk, listed):
-        weight_copy(chunk, listed).wait()
-        blocks[chunk, listed] = jnp.dot(
-            sources[listed], matrices[chunk, listed], preferred_element_type=jnp.float32
-        )
+    batch = 8 if list_total % 8 == 0 else 1
+
+    def compute(chunk, at):
+        members = [at * batch + offset for offset in range(batch)]
+        for listed in members:
+            weight_copy(chunk, listed).wait()
+        products = [
+            jnp.dot(sources[listed], matrices[chunk, listed], preferred_element_type=jnp.float32)
+            for listed in members
+        ]
+        for listed, product in zip(members, products):
+            blocks[chunk, listed] = product
 
     def data_copy(chunk, shift):
         peer = lax.rem(my_face + shift, n_face)
@@ -152,7 +159,7 @@
         return jnp.where(last >= 0, early, 0.0), jnp.where(last > first, late, 0.0)
 
     for chunk in range(chunks):
-        loop(0, list_total, functools.partial(compute, chunk))
+        loop(0, list_total // batch, functools.partial(compute, chunk))
 
         def send(shift):
             peer = lax.rem(my_face + shift, n_face)

time: 20.8 us -> 19.8 us (0.952)
  Pallas kernels: 19.3 us -> 18.4 us
    pallas_call x1, Pallas kernels: 19.3 us -> 18.4 us  [local(): pl.pallas_call(functools.partial(kernel, n_obs, n_face, chunks), out_shap...]
where the time goes in v3:
time: 19.8 us; the launch traced here: 19.6 us
  Pallas kernels  18.4 us (93%)
  between operations  0.66 us (3%)
  local copies, waits for them, and re-layouts  0.62 us (3%)
    pallas_call x1, Pallas kernels, local(): pl.pallas_call(functools.partial(kernel, n_obs, n_face, chunks), out_shap...  18.4 us
    unnamed x1, local copies, waits for them, and re-layouts  0.62 us

profile of v3, /device:TPU:0, one launch (start us, length us, event | category | flops | bytes accessed | tf_op | source)
XLA Modules:
  0.0 19.6 jit_solution(10382385682609894398)
XLA Ops:
  0.7 18.4 %shard_map.91 = f32[32,256]{1,0:T(8,128)S(1)} custom-call(f32[3,1,8]{2,1,0:T(1,128)} %bitcast.1, s32[1,8]{1,0:T(1,128)} %bin_index.1, s32[1,8]{1,0:T(1,128)} %group_index.1, s32[1]{0:T(128)S(6)} %copy.12.item_count, f32[34,256]{1,0:T(8,128)} %density.1, f32[3,34,256]{2,1,0:T(8,128)} %velocity.1, f32[34,256]{1,0:T(8,128)} %pressure.1, f32[3,256]{1,0:T(4,128)} %normal.1, ...), custom_call_target="tpu_custom_call" | custom-call | tf_op jit(solution)/shard_map/pallas_call | solution.py:240
  19.0 0.6 %copy.11 = f32[32,256]{1,0:T(8,128)} copy(f32[32,256]{1,0:T(8,128)S(1)} %shard_map.91) | data formatting | bytes 65536
